TPU v7x, 8 devices: a whole 2x2x1 slice. The times are simulated.
8 devices in a mesh: data: 8 (over z, y, x, core).
Axes of the slice: x: 2, y: 2, z: 1, core: 2. Of those that a mesh axis runs over, the one named last changes fastest.
Arguments:
- x_now: bfloat16 [32, 784, 128], P('data')
- labels_now: int32 [32], P('data')
- x_next: bfloat16 [32, 784, 128], P('data')
- up_one: float32 [2, 128, 512], replicated
- down_one: float32 [2, 512, 128], replicated
- merge_proj: float32 [512, 512], replicated
- up_two: float32 [2, 512, 2048], replicated
- down_two: float32 [2, 2048, 512], replicated
- head_proj: float32 [512, 1000], replicated
- vel_up_one: float32 [2, 128, 512], replicated
- vel_down_one: float32 [2, 512, 128], replicated
- vel_merge_proj: float32 [512, 512], replicated
- vel_up_two: float32 [2, 512, 2048], replicated
- vel_down_two: float32 [2, 2048, 512], replicated
- vel_head_proj: float32 [512, 1000], replicated
Outputs:
- output 1: float32 [32, 1000], P('data')
- output 2: float32 [2, 128, 512], replicated
- output 3: float32 [2, 512, 128], replicated
- output 4: float32 [512, 512], replicated
- output 5: float32 [2, 512, 2048], replicated
- output 6: float32 [2, 2048, 512], replicated
- output 7: float32 [512, 1000], replicated
- output 8: float32 [2, 128, 512], replicated
- output 9: float32 [2, 512, 128], replicated
- output 10: float32 [512, 512], replicated
- output 11: float32 [2, 512, 2048], replicated
- output 12: float32 [2, 2048, 512], replicated
- output 13: float32 [512, 1000], replicated
All inputs are finite; a program needn't handle non-finite values.
Results may differ from a plain program's by a relative error of at most 0.0111885.
Values are sent between devices in bfloat16 or wider.
A program may use at most 1 GiB of HBM per device.

v0:
```python
import jax
import jax.numpy as jnp
from jax import lax
from jax.sharding import PartitionSpec as P

MOMENTUM = 0.9
TRUST = 0.1
LN_EPS = 1e-6


def layer_norm(values):
    row_mean = jnp.mean(values, axis=-1, keepdims=True)
    centered = values - row_mean
    variance = jnp.mean(centered * centered, axis=-1, keepdims=True)
    return centered * lax.rsqrt(variance + LN_EPS)


def gelu_tanh(values):
    return jax.nn.gelu(values, approximate=True)


def contract_rows(lhs_mat, rhs_mat):
    return lax.dot_general(lhs_mat, rhs_mat, (((0,), (0,)), ((), ())), preferred_element_type=jnp.float32)


def contract_cols(lhs_mat, rhs_mat):
    return lax.dot_general(lhs_mat, rhs_mat, (((1,), (1,)), ((), ())), preferred_element_type=jnp.float32)


def to_bf16_layers(stacked):
    return [stacked[layer_num].astype(jnp.bfloat16) for layer_num in range(stacked.shape[0])]


def cast_weights(params):
    up_one, down_one, merge_proj, up_two, down_two, head_proj = params
    return (to_bf16_layers(up_one), to_bf16_layers(down_one), merge_proj.astype(jnp.bfloat16), to_bf16_layers(up_two), to_bf16_layers(down_two), head_proj.astype(jnp.bfloat16))


def block_forward(residual, w_up, w_down):
    normed, norm_back = jax.vjp(layer_norm, residual.astype(jnp.float32))
    normed_b = normed.astype(jnp.bfloat16)
    pre_act = jnp.dot(normed_b, w_up, preferred_element_type=jnp.float32)
    activated, gelu_back = jax.vjp(gelu_tanh, pre_act)
    activated_b = activated.astype(jnp.bfloat16)
    block_out = jnp.dot(activated_b, w_down, preferred_element_type=jnp.float32)
    new_residual = (residual.astype(jnp.float32) + block_out).astype(jnp.bfloat16)
    return new_residual, (normed_b, activated_b, norm_back, gelu_back)


def block_backward(grad_out, saved, w_up, w_down):
    normed_b, activated_b, norm_back, gelu_back = saved
    grad_down = contract_rows(activated_b, grad_out)
    grad_act = contract_cols(grad_out, w_down)
    grad_pre = gelu_back(grad_act)[0].astype(jnp.bfloat16)
    grad_up = contract_rows(normed_b, grad_pre)
    grad_normed = contract_cols(grad_pre, w_up)
    grad_in = norm_back(grad_normed)[0] + grad_out.astype(jnp.float32)
    return grad_in.astype(jnp.bfloat16), grad_up, grad_down


def model_forward(images, weights):
    ups_one, downs_one, merge_w, ups_two, downs_two, head_w = weights
    img_count, tokens, width = images.shape
    residual = images.reshape(img_count * tokens, width)
    saved_one = []
    for w_up, w_down in zip(ups_one, downs_one):
        residual, saved = block_forward(residual, w_up, w_down)
        saved_one.append(saved)
    merged = residual.reshape(img_count * tokens // 4, 4 * width)
    residual = jnp.dot(merged, merge_w, preferred_element_type=jnp.float32).astype(jnp.bfloat16)
    saved_two = []
    for w_up, w_down in zip(ups_two, downs_two):
        residual, saved = block_forward(residual, w_up, w_down)
        saved_two.append(saved)
    pooled = jnp.mean(residual.reshape(img_count, tokens // 4, -1), axis=1, dtype=jnp.float32)
    head_in, head_back = jax.vjp(layer_norm, pooled)
    head_in_b = head_in.astype(jnp.bfloat16)
    logits = jnp.dot(head_in_b, head_w, preferred_element_type=jnp.float32)
    return logits, (saved_one, merged, saved_two, head_in_b, head_back)


def loss_grad(logits, labels, global_batch):
    soft_probs = jax.nn.softmax(logits, axis=-1)
    class_ids = jnp.arange(logits.shape[1], dtype=jnp.int32)
    onehot = (labels[:, None] == class_ids[None, :]).astype(jnp.float32)
    return ((soft_probs - onehot) / global_batch).astype(jnp.bfloat16)


def head_input_grad(grad_logits, head_w, head_back, merged_tokens):
    grad_pooled = head_back(contract_cols(grad_logits, head_w))[0] / merged_tokens
    img_count, width_two = grad_pooled.shape
    spread = jnp.broadcast_to(grad_pooled.astype(jnp.bfloat16)[:, None, :], (img_count, merged_tokens, width_two))
    return spread.reshape(img_count * merged_tokens, width_two)


def lars_step(weight, velocity, grad_sum):
    grad_f = grad_sum.astype(jnp.float32)
    red_axes = (weight.ndim - 2, weight.ndim - 1)
    w_norm = jnp.sqrt(jnp.sum(weight * weight, axis=red_axes, keepdims=True))
    g_norm = jnp.sqrt(jnp.sum(grad_f * grad_f, axis=red_axes, keepdims=True))
    new_vel = MOMENTUM * velocity + TRUST * (w_norm / g_norm) * grad_f
    return weight - new_vel, new_vel


def finish_step(params, velocities, grad_sums, x_next):
    updated = [lars_step(weight, velocity, grad_sum) for weight, velocity, grad_sum in zip(params, velocities, grad_sums)]
    new_params = tuple(pair_new[0] for pair_new in updated)
    new_vels = tuple(pair_new[1] for pair_new in updated)
    logits_next = model_forward(x_next, cast_weights(new_params))[0]
    return (logits_next,) + new_params + new_vels


def solution(mesh):
    data_devs = mesh.shape['data']

    def local_step(x_now, labels_now, x_next, up_one, down_one, merge_proj, up_two, down_two, head_proj, vel_up_one, vel_down_one, vel_merge_proj, vel_up_two, vel_down_two, vel_head_proj):
        params = (up_one, down_one, merge_proj, up_two, down_two, head_proj)
        velocities = (vel_up_one, vel_down_one, vel_merge_proj, vel_up_two, vel_down_two, vel_head_proj)
        weights = cast_weights(params)
        ups_one, downs_one, merge_w, ups_two, downs_two, head_w = weights
        img_count, tokens, width = x_now.shape
        depth_one = len(ups_one)
        depth_two = len(ups_two)
        logits, saved = model_forward(x_now, weights)
        saved_one, merged, saved_two, head_in_b, head_back = saved
        grad_logits = loss_grad(logits, labels_now, img_count * data_devs)
        sum_head = lax.psum(contract_rows(head_in_b, grad_logits).astype(jnp.bfloat16), 'data')
        grad_resid = head_input_grad(grad_logits, head_w, head_back, tokens // 4)
        sums_up_two = [None] * depth_two
        sums_down_two = [None] * depth_two
        for layer_num in reversed(range(depth_two)):
            grad_resid, grad_up, grad_down = block_backward(grad_resid, saved_two[layer_num], ups_two[layer_num], downs_two[layer_num])
            sums_down_two[layer_num] = lax.psum(grad_down.astype(jnp.bfloat16), 'data')
            sums_up_two[layer_num] = lax.psum(grad_up.astype(jnp.bfloat16), 'data')
        sum_merge = lax.psum(contract_rows(merged, grad_resid).astype(jnp.bfloat16), 'data')
        grad_resid = contract_cols(grad_resid, merge_w).astype(jnp.bfloat16).reshape(img_count * tokens, width)
        sums_up_one = [None] * depth_one
        sums_down_one = [None] * depth_one
        for layer_num in reversed(range(depth_one)):
            grad_resid, grad_up, grad_down = block_backward(grad_resid, saved_one[layer_num], ups_one[layer_num], downs_one[layer_num])
            sums_down_one[layer_num] = lax.psum(grad_down.astype(jnp.bfloat16), 'data')
            sums_up_one[layer_num] = lax.psum(grad_up.astype(jnp.bfloat16), 'data')
        grad_sums = (jnp.stack(sums_up_one), jnp.stack(sums_down_one), sum_merge, jnp.stack(sums_up_two), jnp.stack(sums_down_two), sum_head)
        return finish_step(params, velocities, grad_sums, x_next)

    replicated = P()
    batch_split = P('data')
    in_specs = (batch_split, batch_split, batch_split) + (replicated,) * 12
    out_specs = (batch_split,) + (replicated,) * 12
    return jax.shard_map(local_step, mesh=mesh, in_specs=in_specs, out_specs=out_specs, check_vma=False)
```

profile of v0, /device:TPU:0, one launch (start us, length us, event | category | flops | bytes accessed | tf_op | source)
XLA Modules:
  0.0 386.0 jit_solution(18399476972353054816)
XLA Ops:
  7.2 1.5 convert_reduce_fusion.4
  8.7 2.1 multiply_reduce_fusion.6
  10.8 2.0 multiply_convert_fusion.6
  12.9 1.9 multiply_reduce_fusion.10
  16.0 2.4 fusion.228
  19.4 4.7 %multiply_convert_fusion.2 = (bf16[3136,512]{1,0:T(8,128)(2,1)S(1)}, f32[3136,512]{1,0:T(8,128)}) fusion(bf16[2,128,512]{2,1,0:T(8,128)(2,1)S(1)} %get-tuple-element.46, f32[3136,128]{1,0:T(8,128)S(1)} %get-tuple-element.48, f32[3136]{0:T(1024)S(1)} %fusion.177, f32[3136]{0:T(1024)S(1)} %broadcast_multiply_fusion.1), kind=kOutput, calls=%fused_computation.82 | convolution fusion | flops 426696704 | bytes 11403264 | tf_op jit(solution)/shard_map/dot_general | solution.py:42
  24.2 1.7 copy-done.8
  25.9 2.0 fusion.66
  27.8 2.4 reshape.353
  30.3 1.8 convert_reduce_fusion.3
  32.6 8.2 %multiply_reduce_fusion.1 = (f32[2]{0:T(128)}, bf16[2,512,2048]{2,1,0:T(8,128)(2,1)S(1)}) fusion(f32[2,512,2048]{2,1,0:T(8,128)} %param.21), kind=kLoop, calls=%fused_computation.21 | loop fusion | flops 6291454 | bytes 12582920 | tf_op jit(solution)/shard_map/reduce_sum | solution.py:99
  40.8 1.9 fusion.99
  42.7 1.8 slice-done.1
  44.5 2.4 convert_reduce_fusion.2
  47.7 1.9 fusion.101
  49.6 2.7 copy-done.37
  52.3 3.4 fusion.126
  55.8 2.8 reshape.359
  58.5 1.6 reduce_sum.430
  60.4 2.1 fusion.229
  62.7 2.0 multiply_reduce_fusion.12
  65.9 2.6 reshape.354
  68.5 8.2 %fusion.31 = bf16[784,2048]{1,0:T(8,128)(2,1)S(1)} fusion(f32[784,2048]{1,0:T(8,128)} %copy-done.37, bf16[784,512]{1,0:T(8,128)(2,1)} %reshape.354, f32[2,2048,512]{2,1,0:T(8,128)} %param.22), kind=kOutput, calls=%fused_computation.49 | convolution fusion | flops 1676279808 | bytes 12533760 | tf_op jit(solution)/shard_map/dot_general | solution.py:27
  76.8 2.0 fusion.112
  80.1 8.8 %fusion.24 = bf16[784,2048]{1,0:T(8,128)(2,1)S(1)} fusion(f32[784,2048]{1,0:T(8,128)} %copy-done.36, bf16[784,512]{1,0:T(8,128)(2,1)S(1)} %add_convert_fusion.2, f32[2,2048,512]{2,1,0:T(8,128)} %param.22), kind=kOutput, calls=%fused_computation.42 | convolution fusion | flops 1676279808 | bytes 12533760 | tf_op jit(solution)/shard_map/dot_general | solution.py:27
  89.0 2.0 fusion.108
  92.3 1.5 convolution_convert_fusion.8
  93.8 1.5 convolution_convert_fusion.6
  95.5 2.3 reshape.355
  97.8 6.8 %fusion.17 = bf16[3136,512]{1,0:T(8,128)(2,1)S(1)} fusion(f32[3136,512]{1,0:T(8,128)} %get-tuple-element.50, bf16[3136,128]{1,0:T(8,128)(2,1)} %reshape.355, f32[2,512,128]{2,1,0:T(8,128)} %param.19), kind=kOutput, calls=%fused_computation.35 | convolution fusion | flops 443154432 | bytes 10567680 | tf_op jit(solution)/shard_map/dot_general | solution.py:27
  105.8 2.3 fusion.128
  108.1 1.7 fusion.130
  109.9 3.9 %fusion.74 = bf16[1,512,2048]{2,1,0:T(8,128)(2,1)} fusion(bf16[784,2048]{1,0:T(8,128)(2,1)S(1)} %copy-done.35, bf16[784,512]{1,0:T(8,128)(2,1)S(1)} %copy-done.7, f32[784]{0:T(1024)S(1)} %fusion.182, f32[784]{0:T(1024)S(1)} %broadcast_multiply_fusion.7), kind=kOutput, calls=%fused_computation.106 | convolution fusion | flops 1646821376 | bytes 6117504 | tf_op jit(solution)/shard_map/dot_general | solution.py:23
  113.8 3.9 %fusion.75 = bf16[1,512,2048]{2,1,0:T(8,128)(2,1)} fusion(bf16[784,2048]{1,0:T(8,128)(2,1)S(1)} %copy-done.33, bf16[784,512]{1,0:T(8,128)(2,1)S(1)} %copy-done.16, f32[784]{0:T(1024)S(1)} %fusion.183, f32[784]{0:T(1024)S(1)} %broadcast_multiply_fusion.6), kind=kOutput, calls=%fused_computation.107 | convolution fusion | flops 1646821376 | bytes 6117504 | tf_op jit(solution)/shard_map/dot_general | solution.py:23
  117.7 7.5 %fusion.76 = bf16[1,2048,512]{2,1,0:T(8,128)(2,1)} fusion(bf16[784,512]{1,0:T(8,128)(2,1)S(1)} %copy-done.28, f32[784,2048]{1,0:T(8,128)} %copy-done.36), kind=kOutput, calls=%fused_computation.108 | convolution fusion | flops 1659666432 | bytes 9322496 | tf_op jit(solution)/shard_map/dot_general | solution.py:23
  125.2 4.5 %fusion.77 = bf16[1,2048,512]{2,1,0:T(8,128)(2,1)} fusion(bf16[784,512]{1,0:T(8,128)(2,1)S(1)} %copy-done.26, f32[784,2048]{1,0:T(8,128)S(1)} %bitcast.154), kind=kOutput, calls=%fused_computation.109 | convolution fusion | flops 1659666432 | bytes 9322496 | tf_op jit(solution)/shard_map/dot_general | solution.py:23
  129.8 1.5 convolution_convert_fusion.4
  131.3 1.8 fusion.226
  133.6 3.2 fusion.129
  136.8 2.4 fusion.117
  139.2 8.5 %fusion.131 = bf16[1,128,512]{2,1,0:T(8,128)(2,1)} fusion(bf16[3136,128]{1,0:T(8,128)(2,1)} %fusion.117, f32[3136,512]{1,0:T(8,128)} %copy-done.1, bf16[3136,128]{1,0:T(8,128)(2,1)S(1)} %add_convert_fusion, f32[2,512,128]{2,1,0:T(8,128)S(1)} %copy-done.22), kind=kOutput, calls=%fused_computation.204 | convolution fusion | flops 854261760 | bytes 8290304 | tf_op jit(solution)/shard_map/dot_general | solution.py:23
  152.4 1.5 convert_reduce_fusion.5
  153.9 2.1 multiply_reduce_fusion.7
  156.0 2.9 multiply_convert_fusion.7
  158.9 4.6 %multiply_reduce_fusion = f32[2]{0:T(128)S(1)} fusion(f32[2,2048,512]{2,1,0:T(8,128)} %param.22), kind=kLoop, calls=%fused_computation.20 | loop fusion | flops 4194302 | bytes 8388616 | tf_op jit(solution)/shard_map/reduce_sum | solution.py:99
  163.5 125.2 %all-reduce.3.cloned.1.call-done = (bf16[512,1000]{0,1:T(8,128)(2,1)}, bf16[1,2048,512]{2,1,0:T(8,128)(2,1)}, bf16[1,2048,512]{2,1,0:T(8,128)(2,1)}, bf16[1,512,...) async-done(((bf16[512,1000]{0,1:T(8,128)(2,1)}, ...) | async-done | bytes 10461200 | tf_op jit(solution)/shard_map/psum | solution.py:127
  288.7 1.9 fusion.132
  292.5 2.5 fusion.216
  296.2 2.5 fusion.218
  298.7 5.1 %fusion.230 = (f32[3136]{0:T(1024)S(1)}, f32[3136,128]{1,0:T(8,128)}) fusion(bf16[2,512,128]{2,1,0:T(8,128)(2,1)} %get-tuple-element.28, bf16[3136,128]{1,0:T(8,128)(2,1)} %bitcast.152, bf16[2,128,512]{2,1,0:T(8,128)(2,1)S(1)} %get-tuple-element.25, bf16[3136,128]{1,0:T(8,128)(2,1)} %bitcast.150), kind=kOutput, calls=%fused_computation.337 | convolution fusion | flops 838538176 | bytes 3485952 | tf_op jit(solution)/shard_map/dot_general | solution.py:45
  303.8 2.4 multiply_reduce_fusion.3
  306.2 5.9 %fusion.69 = bf16[3136,128]{1,0:T(8,128)(2,1)} fusion(f32[3136,128]{1,0:T(8,128)} %get-tuple-element.66, f32[3136]{0:T(1024)S(1)} %add_rsqrt_fusion, f32[3136]{0:T(1024)S(1)} %broadcast_multiply_fusion, bf16[2,512,128]{2,1,0:T(8,128)(2,1)} %get-tuple-element.28, bf16[2,128,512]{2,1,0:T(8,128)(2,1)S(1)} %get-tuple-element.25), kind=kOutput, calls=%fused_computation.95 | convolution fusion | flops 838541312 | bytes 4308992 | tf_op jit(solution)/shard_map/dot_general | solution.py:45
  312.1 2.3 reshape.356
  314.3 2.8 fusion.214
  317.1 2.2 convert_reduce_fusion.1
  321.2 16.1 %fusion.220 = (bf16[2,512,2048]{2,1,0:T(8,128)(2,1)}, f32[2,512,2048]{2,1,0:T(8,128)}, f32[2,512,2048]{2,1,0:T(8,128)}) fusion(f32[2,512,2048]{2,1,0:T(8,128)} %param.21, bf16[1,512,2048]{2,1,0:T(8,128)(2,1)} %get-tuple-element.16, bf16[1,512,2048]{2,1,0:T(8,128)(2,1)} %get-tuple-element.17, f32[2]{0:T(128)S(1)} %multiply_multiply_fusion.16, ...), kind=kLoop, calls=%fused_computation.330 | loop fusion | flops 14680064 | bytes 41943048 | tf_op jit(solution)/shard_map/convert.7
  337.3 2.5 fusion.2
  339.9 11.6 %fusion.222 = (bf16[2,2048,512]{2,1,0:T(8,128)(2,1)}, f32[2,2048,512]{2,1,0:T(8,128)}, f32[2,2048,512]{2,1,0:T(8,128)}) fusion(f32[2,2048,512]{2,1,0:T(8,128)S(1)} %bitcast.146, bf16[1,2048,512]{2,1,0:T(8,128)(2,1)S(1)} %copy-done.10, bf16[1,2048,512]{2,1,0:T(8,128)(2,1)} %get-tuple-element.15, f32[2]{0:T(128)S(1)} %multiply_multiply_fusion.15, ...), kind=kLoop, calls=%fused_computation.331 | loop fusion | flops 14680064 | bytes 41943048 | tf_op jit(solution)/shard_map/convert.6
  351.5 6.8 %convert_reduce_fusion = (f32[784]{0:T(1024)S(1)}, bf16[784,512]{1,0:T(8,128)(2,1)}) fusion(bf16[2,2048,512]{2,1,0:T(8,128)(2,1)} %get-tuple-element.34, bf16[2,512,2048]{2,1,0:T(8,128)(2,1)} %get-tuple-element.31, bf16[784,512]{1,0:T(8,128)(2,1)S(1)} %get-tuple-element.68, f32[784]{0:T(1024)S(1)} %add_rsqrt_fusion.4, f32[784]{0:T(1024)S(1)} %broadcast_multiply_fusion.5), kind=kOutput, calls=%fused_computation.114 | convolution fusion | flops 3306396928 | bytes 6614080 | tf_op jit(solution)/shard_map/dot_general | solution.py:45
  358.3 1.5 fusion.102
  359.8 7.5 %fusion.123 = f32[784,512]{1,0:T(8,128)} fusion(bf16[2,2048,512]{2,1,0:T(8,128)(2,1)} %get-tuple-element.34, bf16[2,512,2048]{2,1,0:T(8,128)(2,1)} %get-tuple-element.31, bf16[784,512]{1,0:T(8,128)(2,1)} %get-tuple-element.70, f32[784]{0:T(1024)S(1)} %add_rsqrt_fusion.3, f32[784]{0:T(1024)S(1)} %broadcast_multiply_fusion.4), kind=kOutput, calls=%fused_computation.188 | convolution fusion | flops 3305996288 | bytes 7411840 | tf_op jit(solution)/shard_map/dot_general | solution.py:45
  367.4 2.8 reshape.360
  370.2 1.6 reduce_sum.457
  373.9 3.6 fusion.224
  (156 shorter events, 20.0 us)
Async XLA Ops:
  7.2 281.6 %all-reduce.3.cloned.1.call-start = ((), (), s32[]{:S(2)}) async-start(), calls=%async_computation | async-start | bytes 20922368 | tf_op jit(solution)/shard_map/psum | solution.py:127
  14.7 1.1 copy-start.3
  14.7 1.3 copy-start.21
  15.7 2.7 copy-start.1
  24.2 1.7 copy-start.8
  25.9 4.4 %copy-start.2 = (f32[512,512]{1,0:T(8,128)S(1)}, f32[512,512]{1,0:T(8,128)}, u32[]{:S(2)}) copy-start(f32[512,512]{1,0:T(8,128)} %param.20) | copy-start | bytes 3145732
  32.1 10.6 %copy-start.5 = (bf16[784,512]{1,0:T(8,128)(2,1)}, bf16[784,512]{1,0:T(8,128)(2,1)S(1)}, u32[]{:S(2)}) copy-start(bf16[784,512]{1,0:T(8,128)(2,1)S(1)} %get-tuple-element.52) | copy-start | bytes 2408452
  32.6 10.1 %slice-start = ((s8[8388608]{0:T(1024)(128)(4,1)}), s8[4194304]{0:T(1024)(128)(4,1)S(1)}, s32[]{:S(2)}) async-start(s8[8388608]{0:T(1024)(128)(4,1)} %bitcast.143), calls=%async_computation.1 | async-start | bytes 8388608
  40.8 6.9 %copy-start.18 = (bf16[2,512,2048]{2,1,0:T(8,128)(2,1)}, bf16[2,512,2048]{2,1,0:T(8,128)(2,1)S(1)}, u32[]{:S(2)}) copy-start(bf16[2,512,2048]{2,1,0:T(8,128)(2,1)S(1)} %get-tuple-element.44) | copy-start | bytes 12582916
  40.8 3.7 slice-start.1
  44.5 2.7 copy-start.36
  47.2 2.4 copy-start.14
  49.6 2.7 copy-start.37
  55.8 6.9 %copy-start.29 = (s32[4]{0:T(128)S(1)}, s32[4]{0:T(128)}, u32[]{:S(2)}) copy-start(s32[4]{0:T(128)} %param.16) | copy-start | bytes 52
  68.5 8.2 %copy-start.15 = (bf16[784,512]{1,0:T(8,128)(2,1)S(1)}, bf16[784,512]{1,0:T(8,128)(2,1)}, u32[]{:S(2)}) copy-start(bf16[784,512]{1,0:T(8,128)(2,1)} %copy-done.14) | copy-start | bytes 2408452
  68.5 8.3 %copy-start.19 = (bf16[2,512,2048]{2,1,0:T(8,128)(2,1)S(1)}, bf16[2,512,2048]{2,1,0:T(8,128)(2,1)}, u32[]{:S(2)}) copy-start(bf16[2,512,2048]{2,1,0:T(8,128)(2,1)} %copy-done.18) | copy-start | bytes 12582916
  76.8 2.0 copy-start.32
  76.8 2.7 copy-start.25
  80.1 11.6 %copy-start.27 = (bf16[784,512]{1,0:T(8,128)(2,1)}, bf16[784,512]{1,0:T(8,128)(2,1)S(1)}, u32[]{:S(2)}) copy-start(bf16[784,512]{1,0:T(8,128)(2,1)S(1)} %add_convert_fusion.2) | copy-start | bytes 2408452
  80.1 8.8 %copy-start.6 = (bf16[784,512]{1,0:T(8,128)(2,1)S(1)}, bf16[784,512]{1,0:T(8,128)(2,1)}, u32[]{:S(2)}) copy-start(bf16[784,512]{1,0:T(8,128)(2,1)} %copy-done.5) | copy-start | bytes 2408452
  89.0 2.0 copy-start.34
  91.0 1.3 copy-start.24
  105.8 2.3 copy-start.9
  105.8 2.3 copy-start.23
  105.8 4.1 %copy-start.7 = (bf16[784,512]{1,0:T(8,128)(2,1)S(1)}, bf16[784,512]{1,0:T(8,128)(2,1)}, u32[]{:S(2)}) copy-start(bf16[784,512]{1,0:T(8,128)(2,1)} %copy-done.5) | copy-start | bytes 2408452
  105.8 4.1 %copy-start.35 = (bf16[784,2048]{1,0:T(8,128)(2,1)S(1)}, bf16[784,2048]{1,0:T(8,128)(2,1)}, u32[]{:S(2)}) copy-start(bf16[784,2048]{1,0:T(8,128)(2,1)} %copy-done.34) | copy-start | bytes 9633796
  109.9 3.9 %copy-start.16 = (bf16[784,512]{1,0:T(8,128)(2,1)S(1)}, bf16[784,512]{1,0:T(8,128)(2,1)}, u32[]{:S(2)}) copy-start(bf16[784,512]{1,0:T(8,128)(2,1)} %copy-done.14) | copy-start | bytes 2408452
  109.9 3.9 %copy-start.33 = (bf16[784,2048]{1,0:T(8,128)(2,1)S(1)}, bf16[784,2048]{1,0:T(8,128)(2,1)}, u32[]{:S(2)}) copy-start(bf16[784,2048]{1,0:T(8,128)(2,1)} %copy-done.32) | copy-start | bytes 9633796
  113.8 3.9 %copy-start.28 = (bf16[784,512]{1,0:T(8,128)(2,1)S(1)}, bf16[784,512]{1,0:T(8,128)(2,1)}, u32[]{:S(2)}) copy-start(bf16[784,512]{1,0:T(8,128)(2,1)} %copy-done.27) | copy-start | bytes 2408452
  113.8 11.4 %slice-start.6 = ((s8[6422528]{0:T(1024)(128)(4,1)}), s8[4194304]{0:T(1024)(128)(4,1)S(1)}, s32[]{:S(2)}) async-start(s8[6422528]{0:T(1024)(128)(4,1)} %bitcast.153), calls=%async_computation.7 | async-start | bytes 8388608
  117.7 7.5 %copy-start.26 = (bf16[784,512]{1,0:T(8,128)(2,1)S(1)}, bf16[784,512]{1,0:T(8,128)(2,1)}, u32[]{:S(2)}) copy-start(bf16[784,512]{1,0:T(8,128)(2,1)} %reshape.354) | copy-start | bytes 2408452
  117.7 7.5 %slice-start.7 = ((s8[6422528]{0:T(1024)(128)(4,1)}), s8[2228224]{0:T(1024)(128)(4,1)S(1)}, s32[]{:S(2)}) async-start(s8[6422528]{0:T(1024)(128)(4,1)} %bitcast.153), calls=%async_computation.8 | async-start | bytes 4456448
  117.7 15.8 %slice-start.4 = ((s8[6422528]{0:T(1024)(128)(4,1)}), s8[4194304]{0:T(1024)(128)(4,1)S(1)}, s32[]{:S(2)}) async-start(s8[6422528]{0:T(1024)(128)(4,1)} %bitcast.147), calls=%async_computation.5 | async-start | bytes 8388608
  125.2 8.4 %slice-start.5 = ((s8[6422528]{0:T(1024)(128)(4,1)}), s8[2228224]{0:T(1024)(128)(4,1)S(1)}, s32[]{:S(2)}) async-start(s8[6422528]{0:T(1024)(128)(4,1)} %bitcast.147), calls=%async_computation.6 | async-start | bytes 4456448
  133.6 3.2 copy-start.4
  133.6 5.6 %copy-start.22 = (f32[2,512,128]{2,1,0:T(8,128)S(1)}, f32[2,512,128]{2,1,0:T(8,128)}, u32[]{:S(2)}) copy-start(f32[2,512,128]{2,1,0:T(8,128)} %param.19) | copy-start | bytes 1572868
  147.8 1.6 copy-start
  158.9 133.6 %copy-start.31 = (f32[2]{0:T(128)S(1)}, f32[2]{0:T(128)}, u32[]{:S(2)}) copy-start(f32[2]{0:T(128)} %get-tuple-element.45) | copy-start | bytes 28
  314.3 5.5 %copy-start.11 = (bf16[1,512,2048]{2,1,0:T(8,128)(2,1)S(1)}, bf16[1,512,2048]{2,1,0:T(8,128)(2,1)}, u32[]{:S(2)}) copy-start(bf16[1,512,2048]{2,1,0:T(8,128)(2,1)} %get-tuple-element.16) | copy-start | bytes 6291460
  314.3 5.5 %copy-start.12 = (bf16[1,512,2048]{2,1,0:T(8,128)(2,1)S(1)}, bf16[1,512,2048]{2,1,0:T(8,128)(2,1)}, u32[]{:S(2)}) copy-start(bf16[1,512,2048]{2,1,0:T(8,128)(2,1)} %get-tuple-element.17) | copy-start | bytes 6291460
  317.1 4.0 %copy-start.17 = (f32[512,512]{1,0:T(8,128)}, f32[512,512]{1,0:T(8,128)S(1)}, u32[]{:S(2)}) copy-start(f32[512,512]{1,0:T(8,128)S(1)} %get-tuple-element.23) | copy-start | bytes 3145732
  317.1 4.0 %copy-start.30 = (f32[2]{0:T(128)S(1)}, f32[2]{0:T(128)}, u32[]{:S(2)}) copy-start(f32[2]{0:T(128)} %get-tuple-element.43) | copy-start | bytes 28
  321.2 18.7 %slice-start.2 = ((s8[8388608]{0:T(1024)(128)(4,1)}), s8[4194304]{0:T(1024)(128)(4,1)S(1)}, s32[]{:S(2)}) async-start(s8[8388608]{0:T(1024)(128)(4,1)} %bitcast.145), calls=%async_computation.3 | async-start | bytes 8388608
  321.2 16.2 %copy-start.10 = (bf16[1,2048,512]{2,1,0:T(8,128)(2,1)S(1)}, bf16[1,2048,512]{2,1,0:T(8,128)(2,1)}, u32[]{:S(2)}) copy-start(bf16[1,2048,512]{2,1,0:T(8,128)(2,1)} %get-tuple-element.14) | copy-start | bytes 6291460
  321.2 18.7 %slice-start.3 = ((s8[8388608]{0:T(1024)(128)(4,1)}), s8[4194304]{0:T(1024)(128)(4,1)S(1)}, s32[]{:S(2)}) async-start(s8[8388608]{0:T(1024)(128)(4,1)} %bitcast.145), calls=%async_computation.4 | async-start | bytes 8388608
  367.4 4.7 %copy-start.20 = (bf16[512,1000]{0,1:T(8,128)(2,1)S(1)}, bf16[512,1000]{0,1:T(8,128)(2,1)}, u32[]{:S(2)}) copy-start(bf16[512,1000]{0,1:T(8,128)(2,1)} %get-tuple-element.13) | copy-start | bytes 3072004
  377.6 1.3 copy-start.13
Sparse Core Ops, SparseCore 0:
  147.9 140.7 all-reduce.2
where the time goes:
time: 393 us; the launch traced here: 386 us
  waiting for transfers between devices  125 us (32%)
  matrix products  124 us (32%)
  other arithmetic  96 us (24%)
  local copies, waits for them, and re-layouts  23.3 us (6%)
  between operations  17.7 us (5%)
    psum x1, waiting for transfers between devices, local_step(): lax.psum(contract_rows(head_in_b, grad_logits).astype(jnp.bfloat16), 'data')  125 us
    dot_general x10, matrix products, contract_rows(): lax.dot_general(lhs_mat, rhs_mat, (((0,), (0,)), ((), ())), preferred_ele...  38.6 us
    dot_general x8, matrix products, block_forward(): block_out = jnp.dot(activated_b, w_down, preferred_element_type=jnp.float32)  35.6 us
    another operation x4, other arithmetic  32.8 us
    dot_general x8, matrix products, contract_cols(): lax.dot_general(lhs_mat, rhs_mat, (((1,), (1,)), ((), ())), preferred_ele...  32.5 us
    reduce_sum x6, other arithmetic, lars_step(): w_norm = jnp.sqrt(jnp.sum(weight * weight, axis=red_axes, keepdims=True))  17.8 us
    reduce_sum x10, other arithmetic, layer_norm(): variance = jnp.mean(centered * centered, axis=-1, keepdims=True)  10.7 us
    dot_general x4, matrix products, block_forward(): pre_act = jnp.dot(normed_b, w_up, preferred_element_type=jnp.float32)  9.49 us
  transfers between devices with their start and end apart: 1, of which 1 were waited for; matrix products, arithmetic and copies ran while one was open for 4% of the time, Pallas kernels for 0%

commit v1 on v0

v1 whole, which is shorter than its diff:
```python
import jax
import jax.numpy as jnp
from jax import lax
from jax.experimental import pallas as pl
from jax.experimental.pallas import tpu as pltpu
from jax.sharding import PartitionSpec as P

MOMENTUM = 0.9
TRUST = 0.1
LN_EPS = 1e-6
GELU_A = 0.7978845608028654
GELU_B = 0.044715 * GELU_A
F32 = jnp.float32
BF16 = jnp.bfloat16
VMEM_BYTES = 62 * 1024 * 1024

IMGS, TOKENS, WIDTH = 4, 784, 128
MERGED = TOKENS // 4
ROWS = IMGS * MERGED
WIDE = 4 * WIDTH
HID_ONE, HID_TWO = 4 * WIDTH, 4 * WIDE
CLASSES = 1000
TILE = 256
N_TILES = HID_TWO // TILE
FWD_TILE = 512


def dot_nn(a, b):
    return lax.dot_general(a, b, (((1,), (0,)), ((), ())), preferred_element_type=F32)


def dot_nt(a, b):
    return lax.dot_general(a, b, (((1,), (1,)), ((), ())), preferred_element_type=F32)


def dot_tn(a, b):
    return lax.dot_general(a, b, (((0,), (0,)), ((), ())), preferred_element_type=F32)


def norm_parts(vals):
    centered = vals - jnp.mean(vals, axis=-1, keepdims=True)
    variance = jnp.mean(centered * centered, axis=-1, keepdims=True)
    rstd = lax.rsqrt(variance + LN_EPS)
    return centered * rstd, rstd


def norm_back(grad, normed, rstd):
    mean_g = jnp.mean(grad, axis=-1, keepdims=True)
    mean_gn = jnp.mean(grad * normed, axis=-1, keepdims=True)
    return rstd * (grad - mean_g - normed * mean_gn)


def gelu_parts(pre):
    square = pre * pre
    half = 0.5 * jnp.tanh(pre * (GELU_A + GELU_B * square)) + 0.5
    return square, half


def gelu_slope(pre, square, half):
    return half * (1.0 + pre * (1.0 - half) * (2.0 * GELU_A + 6.0 * GELU_B * square))


def cast_rows(dst, src, rows, step):
    def body(i, carry):
        sl = pl.ds(pl.multiple_of(i * step, step), step)
        dst[sl, :] = src[sl, :].astype(BF16)
        return carry
    lax.fori_loop(0, rows // step, body, 0)


def lanes(index, size):
    return pl.ds(pl.multiple_of(index * size, size), size)


def permute_tokens(x_ref, x_f32, r0):
    x_f32[...] = x_ref[...].astype(F32)
    for j in range(4):
        r0[:, j * WIDTH:(j + 1) * WIDTH] = x_f32[pl.ds(j, ROWS, stride=4), :].astype(BF16)


def stage_one_block(resid, w_up, w_down):
    res_f = resid.astype(F32)
    normed = norm_parts(res_f)[0].astype(BF16)
    pre = dot_nn(normed, w_up)
    act = (pre * gelu_parts(pre)[1]).astype(BF16)
    return (res_f + dot_nn(act, w_down)).astype(BF16)


def stage_one_forward(r0, r1, r2, up_one, down_one):
    def body(j, carry):
        sl = lanes(j, WIDTH)
        mid = stage_one_block(r0[:, sl], up_one[0], down_one[0])
        r1[:, sl] = mid
        r2[:, sl] = stage_one_block(mid, up_one[1], down_one[1])
        return carry
    lax.fori_loop(0, 4, body, 0)


def stage_two_block(src, dst, normed_ref, acc, up_ref, down_ref):
    res_f = src[...].astype(F32)
    normed_ref[...] = norm_parts(res_f)[0].astype(BF16)
    acc[...] = res_f

    def body(t, carry):
        sl = lanes(t, FWD_TILE)
        pre = dot_nn(normed_ref[...], up_ref[:, sl])
        act = (pre * gelu_parts(pre)[1]).astype(BF16)
        acc[...] += dot_nn(act, down_ref[sl, :])
        return carry
    lax.fori_loop(0, HID_TWO // FWD_TILE, body, 0)
    dst[...] = acc[...].astype(BF16)


def image_rows():
    image = lax.broadcasted_iota(jnp.int32, (8, ROWS), 0)
    row = lax.broadcasted_iota(jnp.int32, (8, ROWS), 1)
    inside = (row >= image * MERGED) & (row < (image + 1) * MERGED)
    return jnp.where(inside, 1.0, 0.0).astype(BF16)


def pooled_norm(resid):
    pooled = dot_nn(image_rows(), resid) * (1.0 / MERGED)
    return norm_parts(pooled)


def train_kernel(x_hbm, labels_ref, up1_hbm, dn1_hbm, mg_hbm, up2_hbm, dn2_hbm, hd_hbm,
                 g_up1, g_dn1, g_mg, g_up2, g_dn2, g_hd,
                 x_v, x_f32, st_up1, st_dn1, st_mg, st_up2, st_dn2, st_hd,
                 up1, dn1, mg, up2, dn2, hd,
                 r0, r1, r2, s0, s1, s2, normed_ref, acc, grad_a, grad_b, sems,
                 du1, dv1):
    copies = [pltpu.make_async_copy(src, dst, sems.at[i]) for i, (src, dst) in enumerate((
        (x_hbm, x_v), (up1_hbm, st_up1), (dn1_hbm, st_dn1), (mg_hbm, st_mg),
        (up2_hbm.at[0], st_up2.at[0]), (dn2_hbm.at[0], st_dn2.at[0]),
        (up2_hbm.at[1], st_up2.at[1]), (dn2_hbm.at[1], st_dn2.at[1]), (hd_hbm, st_hd)))]
    for copy in copies:
        copy.start()
    copies[0].wait()
    permute_tokens(x_v, x_f32, r0)
    copies[1].wait()
    copies[2].wait()
    for n in range(2):
        cast_rows(up1.at[n], st_up1.at[n], 128, 64)
        cast_rows(dn1.at[n], st_dn1.at[n], 512, 256)
    stage_one_forward(r0, r1, r2, up1, dn1)
    copies[3].wait()
    cast_rows(mg, st_mg, 512, 64)
    s0[...] = dot_nn(r2[...], mg[...]).astype(BF16)
    for n, (src, dst) in enumerate(((s0, s1), (s1, s2))):
        copies[4 + 2 * n].wait()
        copies[5 + 2 * n].wait()
        cast_rows(up2.at[n], st_up2.at[n], 512, 16)
        cast_rows(dn2.at[n], st_dn2.at[n], 2048, 64)
        stage_two_block(src, dst, normed_ref, acc, up2.at[n], dn2.at[n])
    copies[8].wait()
    cast_rows(hd, st_hd, 512, 64)
    head_normed, head_rstd = pooled_norm(s2[...])
    head_b = head_normed.astype(BF16)
    logits = dot_nn(head_b, hd[...])
    top = jnp.max(logits, axis=-1, keepdims=True)
    expd = jnp.exp(logits - top)
    probs = expd / jnp.sum(expd, axis=-1, keepdims=True)
    class_id = lax.broadcasted_iota(jnp.int32, (8, CLASSES), 1)
    real_row = lax.broadcasted_iota(jnp.int32, (8, CLASSES), 0) < IMGS
    onehot = jnp.where(class_id == labels_ref[...], 1.0, 0.0)
    grad_logits = jnp.where(real_row, (probs - onehot) * (1.0 / 32.0), 0.0).astype(BF16)
    g_hd[...] = dot_tn(head_b, grad_logits).astype(BF16)
    grad_pooled = norm_back(dot_nt(grad_logits, hd[...]), head_normed, head_rstd) * (1.0 / MERGED)
    grad_a[...] = dot_tn(image_rows(), grad_pooled.astype(BF16)).astype(BF16)

    grads = (grad_a, grad_b)
    for step, n in enumerate((1, 0)):
        g_in, g_out = grads[step], grads[1 - step]
        src = (s0, s1)[n]
        normed_f, rstd = norm_parts(src[...].astype(F32))
        normed_ref[...] = normed_f.astype(BF16)

        acc[...] = jnp.zeros_like(acc)

        def body(t, carry, n=n, g_in=g_in):
            sl = lanes(t, TILE)
            pre = dot_nn(normed_ref[...], up2[n, :, sl])
            square, half = gelu_parts(pre)
            act = (pre * half).astype(BF16)
            grad_pre = (gelu_slope(pre, square, half) * dot_nt(g_in[...], dn2[n, sl, :])).astype(BF16)
            g_dn2[n, sl, :] = dot_tn(act, g_in[...]).astype(BF16)
            g_up2[n, :, sl] = dot_tn(normed_ref[...], grad_pre).astype(BF16)
            acc[...] += dot_nt(grad_pre, up2[n, :, sl])
            return carry
        lax.fori_loop(0, N_TILES, body, 0)
        normed_f, rstd = norm_parts(src[...].astype(F32))
        g_out[...] = (norm_back(acc[...], normed_f, rstd) + g_in[...].astype(F32)).astype(BF16)
    g_mg[...] = dot_tn(r2[...], grad_a[...]).astype(BF16)
    grad_b[...] = dot_nt(grad_a[...], mg[...]).astype(BF16)

    for n, src, g_in, g_out in ((1, r1, grad_b, grad_a), (0, r0, grad_a, grad_b)):
        du1[...] = jnp.zeros_like(du1)
        dv1[...] = jnp.zeros_like(dv1)

        def body(j, carry, n=n, src=src, g_in=g_in, g_out=g_out):
            sl = lanes(j, WIDTH)
            normed_f, rstd = norm_parts(src[:, sl].astype(F32))
            normed = normed_f.astype(BF16)
            grad = g_in[:, sl]
            pre = dot_nn(normed, up1[n])
            square, half = gelu_parts(pre)
            act = (pre * half).astype(BF16)
            grad_pre = (gelu_slope(pre, square, half) * dot_nt(grad, dn1[n])).astype(BF16)
            dv1[...] += dot_tn(grad, act)
            du1[...] += dot_tn(normed, grad_pre)
            if n:
                back = norm_back(dot_nt(grad_pre, up1[n]), normed_f, rstd)
                g_out[:, sl] = (back + grad.astype(F32)).astype(BF16)
            return carry
        lax.fori_loop(0, 4, body, 0)
        g_up1[n] = du1[...].astype(BF16)
        g_dn1[n] = dv1[...].T.astype(BF16)


def sum_rows(tile):
    rows, cols = tile.shape
    return jnp.sum(tile.reshape(rows // 8, 8, cols), axis=0)


def lars_matrix(w_ref, v_ref, g_ref, b_ref, step):
    rows, cols = w_ref.shape
    zero = jnp.zeros((8, cols), F32)

    def norms(i, carry):
        sl = pl.ds(pl.multiple_of(i * step, step), step)
        w = w_ref[sl, :]
        g = g_ref[sl, :].astype(F32)
        return carry[0] + sum_rows(w * w), carry[1] + sum_rows(g * g)
    w_acc, g_acc = lax.fori_loop(0, rows // step, norms, (zero, zero))
    w_norm = jnp.sqrt(jnp.sum(jnp.sum(w_acc, axis=0, keepdims=True), axis=1, keepdims=True))
    g_norm = jnp.sqrt(jnp.sum(jnp.sum(g_acc, axis=0, keepdims=True), axis=1, keepdims=True))
    scale = TRUST * (w_norm / g_norm)

    def update(i, carry):
        sl = pl.ds(pl.multiple_of(i * step, step), step)
        new_v = MOMENTUM * v_ref[sl, :] + scale * g_ref[sl, :].astype(F32)
        new_w = w_ref[sl, :] - new_v
        v_ref[sl, :] = new_v
        w_ref[sl, :] = new_w
        b_ref[sl, :] = new_w.astype(BF16)
        return carry
    lax.fori_loop(0, rows // step, update, 0)


def next_kernel(x_hbm, up1_hbm, dn1_hbm, mg_hbm, up2_hbm, dn2_hbm, hd_hbm,
                vup1_hbm, vdn1_hbm, vmg_hbm, vup2_hbm, vdn2_hbm, vhd_hbm,
                gup1_hbm, gdn1_hbm, gmg_hbm, gup2_hbm, gdn2_hbm, ghd_hbm,
                logits_ref, o_up1, o_dn1, o_mg, o_up2, o_dn2, o_hd, ov_up1, ov_dn1, ov_mg, ov_up2, ov_dn2, ov_hd,
                x_v, x_f32, wb_up1, wb_dn1, wb_mg, wb_up2, wb_dn2, wb_hd, vb_up1, vb_dn1, vb_mg, vb_up2, vb_dn2, vb_hd,
                gb_up1, gb_dn1, gb_mg, gb_up2, gb_dn2, gb_hd,
                up1, dn1, mg, up2, dn2, hd, r0, s0, s1, normed_ref, acc, sem_in, sem_out, sem_x):
    jobs = []
    for n in range(2):
        jobs.append((up1_hbm.at[n], vup1_hbm.at[n], gup1_hbm.at[n], o_up1.at[n], ov_up1.at[n],
                     wb_up1.at[n], vb_up1.at[n], gb_up1.at[n], up1.at[n], 64, None))
        jobs.append((dn1_hbm.at[n], vdn1_hbm.at[n], gdn1_hbm.at[n], o_dn1.at[n], ov_dn1.at[n],
                     wb_dn1.at[n], vb_dn1.at[n], gb_dn1.at[n], dn1.at[n], 128, None))
    jobs.append((mg_hbm, vmg_hbm, gmg_hbm, o_mg, ov_mg, wb_mg, vb_mg, gb_mg, mg, 64, None))
    for n in range(2):
        jobs.append((up2_hbm.at[n], vup2_hbm.at[n], gup2_hbm.at[n], o_up2.at[n], ov_up2.at[n],
                     wb_up2, vb_up2, gb_up2, up2, 16, 5 if n else None))
        jobs.append((dn2_hbm.at[n], vdn2_hbm.at[n], gdn2_hbm.at[n], o_dn2.at[n], ov_dn2.at[n],
                     wb_dn2, vb_dn2, gb_dn2, dn2, 64, 6 if n else None))
    jobs.append((hd_hbm, vhd_hbm, ghd_hbm, o_hd, ov_hd, wb_hd, vb_hd, gb_hd, hd, 32, None))

    def loads(k):
        w, v, g, _, _, wb, vb, gb, _, _, _ = jobs[k]
        return [pltpu.make_async_copy(src, dst, sem_in.at[k, i])
                for i, (src, dst) in enumerate(((w, wb), (v, vb), (g, gb)))]

    def stores(k):
        _, _, _, ow, ov, wb, vb, _, _, _, _ = jobs[k]
        return [pltpu.make_async_copy(src, dst, sem_out.at[k, i]) for i, (src, dst) in enumerate(((wb, ow), (vb, ov)))]

    def run(k):
        for copy in loads(k):
            copy.wait()
        _, _, _, _, _, wb, vb, gb, b, step, _ = jobs[k]
        lars_matrix(wb, vb, gb, b, step)
        for copy in stores(k):
            copy.start()

    x_copy = pltpu.make_async_copy(x_hbm, x_v, sem_x)
    x_copy.start()
    for k in (0, 1, 2, 3, 4, 5, 6, 9):
        for copy in loads(k):
            copy.start()

    def reload(k, old):
        for copy in stores(old):
            copy.wait()
        for copy in loads(k):
            copy.start()

    x_copy.wait()
    permute_tokens(x_v, x_f32, r0)
    for k in range(4):
        run(k)
    stage_one_forward(r0, s0, s1, up1, dn1)
    run(4)
    s0[...] = dot_nn(s1[...], mg[...]).astype(BF16)
    run(5)
    run(6)
    stage_two_block(s0, s1, normed_ref, acc, up2, dn2)
    reload(7, 5)
    reload(8, 6)
    run(9)
    run(7)
    run(8)
    stage_two_block(s1, s0, normed_ref, acc, up2, dn2)
    head_b = pooled_norm(s0[...])[0].astype(BF16)
    logits_ref[...] = dot_nn(head_b, hd[...])[:IMGS]
    for k in (0, 1, 2, 3, 4, 9, 7, 8):
        for copy in stores(k):
            copy.wait()


W_SHAPES = ((2, 128, 512), (2, 512, 128), (512, 512), (2, 512, 2048), (2, 2048, 512), (512, 1000))
BIG_SHAPES = W_SHAPES[:3] + ((512, 2048), (2048, 512), (512, 1000))


def vmem(shape, dtype):
    return pltpu.VMEM(shape, dtype)


ANY_SPEC = pl.BlockSpec(memory_space=pl.ANY)
VMEM_SPEC = pl.BlockSpec(memory_space=pltpu.VMEM)


def run_train(x_now, labels, params):
    act = lambda dt=BF16: vmem((ROWS, WIDE), dt)
    return pl.pallas_call(
        train_kernel,
        out_shape=[jax.ShapeDtypeStruct(shape, BF16) for shape in W_SHAPES],
        in_specs=[ANY_SPEC, VMEM_SPEC] + [ANY_SPEC] * 6,
        out_specs=[VMEM_SPEC] * 6,
        scratch_shapes=[vmem((ROWS * 4, WIDTH), BF16), vmem((ROWS * 4, WIDTH), F32)]
        + [vmem(shape, F32) for shape in W_SHAPES] + [vmem(shape, BF16) for shape in W_SHAPES]
        + [act()] * 7 + [act(F32), act(), act(), pltpu.SemaphoreType.DMA((9,)), vmem((128, 512), F32), vmem((128, 512), F32)],
        compiler_params=pltpu.CompilerParams(vmem_limit_bytes=VMEM_BYTES),
        cost_estimate=pl.CostEstimate(flops=30_000_000_000, bytes_accessed=40_000_000, transcendentals=0),
        name='train_part',
    )(x_now, labels, *params)


def run_next(x_next, params, velocities, grads):
    act = lambda dt=BF16: vmem((ROWS, WIDE), dt)
    outs = [jax.ShapeDtypeStruct((IMGS, CLASSES), F32)] + [jax.ShapeDtypeStruct(shape, F32) for shape in W_SHAPES] * 2
    return pl.pallas_call(
        next_kernel,
        out_shape=outs,
        in_specs=[ANY_SPEC] * 19,
        out_specs=[VMEM_SPEC] + [ANY_SPEC] * 12,
        scratch_shapes=[vmem((ROWS * 4, WIDTH), BF16), vmem((ROWS * 4, WIDTH), F32)]
        + [vmem(shape, F32) for shape in BIG_SHAPES] * 2 + [vmem(shape, BF16) for shape in BIG_SHAPES] * 2
        + [act()] * 4 + [act(F32), pltpu.SemaphoreType.DMA((10, 3)), pltpu.SemaphoreType.DMA((10, 2)), pltpu.SemaphoreType.DMA],
        compiler_params=pltpu.CompilerParams(vmem_limit_bytes=VMEM_BYTES),
        cost_estimate=pl.CostEstimate(flops=10_000_000_000, bytes_accessed=100_000_000, transcendentals=0),
        name='next_part',
    )(x_next, *params, *velocities, *grads)


def solution(mesh):
    def local_step(x_now, labels_now, x_next, *weights):
        params, velocities = weights[:6], weights[6:]
        labels = jnp.pad(labels_now, (0, 8 - IMGS)).reshape(8, 1)
        grads = run_train(x_now.reshape(ROWS * 4, WIDTH), labels, params)
        sums = lax.psum(tuple(grads), 'data')
        return tuple(run_next(x_next.reshape(ROWS * 4, WIDTH), params, velocities, sums))

    split = P('data')
    in_specs = (split, split, split) + (P(),) * 12
    out_specs = (split,) + (P(),) * 12
    return jax.shard_map(local_step, mesh=mesh, in_specs=in_specs, out_specs=out_specs, check_vma=False)
```

time: 393 us -> 282 us (0.72); the launches traced: 386 us -> 282 us
  matrix products: 124 us -> 0 us
  Pallas kernels: 0 us -> 118 us
  other arithmetic: 96 us -> 0 us
  waiting for transfers between devices: 125 us -> 137 us
  local copies, waits for them, and re-layouts: 23.3 us -> 12.4 us
    dot_general x34 -> x0, matrix products: 124 us -> none  [the longest x10 38.6 us: contract_rows(): lax.dot_general(lhs_mat, rhs_mat, (((0,), (0,)), ((), ())), preferred_ele...]
    pallas_call x0 -> x2, Pallas kernels: none -> 118 us  [the longest x1 71.9 us: run_train(): pl.pallas_call(train_kernel, out_shape=[jax.ShapeDtypeStruct(shape, BF16)...]
    reduce_sum x33 -> x0, other arithmetic: 47.5 us -> none  [the longest x6 17.8 us: lars_step(): w_norm = jnp.sqrt(jnp.sum(weight * weight, axis=red_axes, keepdims=True))]
    another operation x4 -> x0, other arithmetic: 32.8 us -> none
    psum x1, waiting for transfers between devices: 125 us -> 137 us  [local_step(): sums = lax.psum(tuple(grads), 'data')]
    convert_element_type x7 -> x0, other arithmetic: 9.06 us -> none  [the longest x3 7.32 us: block_forward(): normed_b = normed.astype(jnp.bfloat16)]
    reshape x4 -> x2, local copies, waits for them, and re-layouts: 9.55 us -> 1.33 us  [local_step(): labels = jnp.pad(labels_now, (0, 8 - IMGS)).reshape(8, 1)]
    sub x2 -> x0, other arithmetic: 6.43 us -> none  [lars_step(): return (weight - new_vel, new_vel)]
  transfers between devices with their start and end apart: 1 -> 1, of which waited for: 1 -> 1; matrix products, arithmetic and copies ran while one was open for 4% -> 1% of each run, Pallas kernels for 0% -> 0%
where the time goes in v1:
time: 282 us
  waiting for transfers between devices  137 us (49%)
  Pallas kernels  118 us (42%)
  between operations  14.1 us (5%)
  local copies, waits for them, and re-layouts  12.4 us (4%)
    psum x1, waiting for transfers between devices, local_step(): sums = lax.psum(tuple(grads), 'data')  137 us
    pallas_call x1, Pallas kernels, run_train(): pl.pallas_call(train_kernel, out_shape=[jax.ShapeDtypeStruct(shape, BF16)...  71.9 us
    pallas_call x1, Pallas kernels, run_next(): pl.pallas_call(next_kernel, out_shape=outs, in_specs=[ANY_SPEC] * 19, out...  46.4 us
    unnamed x6, local copies, waits for them, and re-layouts  6.3 us
  transfers between devices with their start and end apart: 1, of which 1 were waited for; matrix products, arithmetic and copies ran while one was open for 1% of the time, Pallas kernels for 0%

profile of v1, /device:TPU:0, one launch (start us, length us, event | category | flops | bytes accessed | tf_op | source)
XLA Modules:
  0.0 282.1 jit_solution(6137311799458869464)
XLA Ops:
  7.2 0.0 all-reduce.4.cloned.1.call-start
  7.2 0.7 pad_bitcast_fusion
  7.9 0.7 copy.28.labels_ref
  8.6 2.9 %copy.30.hd_hbm = f32[512,1000]{1,0:T(8,128)} copy(f32[512,1000]{0,1:T(8,128)} %param.23) | data formatting | bytes 4096000 | tf_op args[8]
  11.5 71.9 %train_part.1 = (bf16[2,128,512]{2,1,0:T(8,128)(2,1)}, bf16[2,512,128]{2,1,0:T(8,128)(2,1)}, bf16[512,512]{1,0:T(8,128)(2,1)}, bf16[2,512,2048]{2,1,0:T(8,128)(2...) custom-call(bf16[3136,128]{1,0:T(8,128)(2,1)} %bitcast.5, s32[8,1]{1,0:T(8,128)} %copy.28.labels_ref, ...), custom_call_target="tpu_custom_call" | custom-call | flops 30000001024 | bytes 40000000 | tf_op jit(solution)/shard_map/train_part/pallas_call | solution.py:337
  83.3 0.0 copy-start.1
  83.3 0.0 all-reduce.4.cloned.1.call-update
  83.4 1.5 copy-done.1
  84.9 1.8 copy.31.vhd_hbm
  86.8 137.4 %all-reduce.4.cloned.1.call-done = (bf16[2,128,512]{2,1,0:T(8,128)(2,1)}, bf16[2,512,128]{2,1,0:T(8,128)(2,1)}, bf16[512,512]{1,0:T(8,128)(2,1)}, bf16[2,512,204...) async-done(((bf16[2,128,512]{2,1,0:T(8,128)(2,1)}, bf16[2,512,128]{2,1,0:T(8,128)(2,1)}, bf16[512,512]{1,0:T(8,128)(2,1)}, ...) | async-done | bytes 10461200 | tf_op jit(solution)/shard_map/psum | solution.py:373
  224.1 46.4 %next_part.1 = (f32[4,1000]{1,0:T(4,128)}, f32[2,128,512]{2,1,0:T(8,128)}, f32[2,512,128]{2,1,0:T(8,128)}, f32[512,512]{1,0:T(8,128)}, f32[2,512,2048]{2,1,0:T(8...) custom-call(bf16[3136,128]{1,0:T(8,128)(2,1)} %bitcast.4, ...), custom_call_target="tpu_custom_call" | custom-call | flops 10000000000 | bytes 100000000 | tf_op jit(solution)/shard_map/next_part/pallas_call | solution.py:354
  270.5 0.0 copy-start
  270.5 3.0 %copy.32 = f32[512,1000]{0,1:T(8,128)} copy(f32[512,1000]{1,0:T(8,128)} %get-tuple-element.31) | data formatting | bytes 4096000 | tf_op jit(solution)/shard_map/next_part/pallas_call | solution.py:354
  273.5 0.0 copy-done
  273.5 1.8 copy.33
Async XLA Ops:
  7.2 216.9 %all-reduce.4.cloned.1.call-start = ((), (), s32[]{:S(2)}) async-start(), calls=%async_computation | async-start | bytes 20971520 | tf_op jit(solution)/shard_map/psum | solution.py:373
  83.3 1.6 copy-start.1
  270.5 3.0 %copy-start = (f32[512,1000]{1,0:T(8,128)S(1)}, f32[512,1000]{1,0:T(8,128)}, u32[]{:S(2)}) copy-start(f32[512,1000]{1,0:T(8,128)} %get-tuple-element.37) | copy-start | bytes 6144004
Sparse Core Ops, SparseCore 0:
  83.5 140.5 all-reduce.3

commit v2 on v1

v2 whole, which is shorter than its diff:
```python
import jax
import jax.numpy as jnp
from jax import lax
from jax.experimental import pallas as pl
from jax.experimental.pallas import tpu as pltpu
from jax.sharding import PartitionSpec as P

MOMENTUM = 0.9
TRUST = 0.1
LN_EPS = 1e-6
GELU_A = 0.7978845608028654
GELU_B = 0.044715 * GELU_A
F32 = jnp.float32
BF16 = jnp.bfloat16
VMEM_BYTES = 62 * 1024 * 1024

IMGS, TOKENS, WIDTH = 4, 784, 128
MERGED = TOKENS // 4
ROWS = IMGS * MERGED
WIDE = 4 * WIDTH
HID_ONE, HID_TWO = 4 * WIDTH, 4 * WIDE
CLASSES = 1000
TILE = 256
SHARD = 64
N_TILES = HID_TWO // TILE
FWD_TILE = 512


def dot_nn(a, b):
    return lax.dot_general(a, b, (((1,), (0,)), ((), ())), preferred_element_type=F32)


def dot_nt(a, b):
    return lax.dot_general(a, b, (((1,), (1,)), ((), ())), preferred_element_type=F32)


def dot_tn(a, b):
    return lax.dot_general(a, b, (((0,), (0,)), ((), ())), preferred_element_type=F32)


def norm_parts(vals):
    centered = vals - jnp.mean(vals, axis=-1, keepdims=True)
    variance = jnp.mean(centered * centered, axis=-1, keepdims=True)
    rstd = lax.rsqrt(variance + LN_EPS)
    return centered * rstd, rstd


def norm_back(grad, normed, rstd):
    mean_g = jnp.mean(grad, axis=-1, keepdims=True)
    mean_gn = jnp.mean(grad * normed, axis=-1, keepdims=True)
    return rstd * (grad - mean_g - normed * mean_gn)


def gelu_parts(pre):
    square = pre * pre
    half = 0.5 * jnp.tanh(pre * (GELU_A + GELU_B * square)) + 0.5
    return square, half


def gelu_slope(pre, square, half):
    return half * (1.0 + pre * (1.0 - half) * (2.0 * GELU_A + 6.0 * GELU_B * square))


def cast_rows(dst, src, rows, step):
    def body(i, carry):
        sl = pl.ds(pl.multiple_of(i * step, step), step)
        dst[sl, :] = src[sl, :].astype(BF16)
        return carry
    lax.fori_loop(0, rows // step, body, 0)


def lanes(index, size):
    return pl.ds(pl.multiple_of(index * size, size), size)


def permute_tokens(x_ref, x_f32, r0):
    x_f32[...] = x_ref[...].astype(F32)
    for j in range(4):
        r0[:, j * WIDTH:(j + 1) * WIDTH] = x_f32[pl.ds(j, ROWS, stride=4), :].astype(BF16)


def stage_one_block(resid, w_up, w_down):
    res_f = resid.astype(F32)
    normed = norm_parts(res_f)[0].astype(BF16)
    pre = dot_nn(normed, w_up)
    act = (pre * gelu_parts(pre)[1]).astype(BF16)
    return (res_f + dot_nn(act, w_down)).astype(BF16)


def stage_one_forward(r0, r1, r2, up_one, down_one):
    def body(j, carry):
        sl = lanes(j, WIDTH)
        mid = stage_one_block(r0[:, sl], up_one[0], down_one[0])
        r1[:, sl] = mid
        r2[:, sl] = stage_one_block(mid, up_one[1], down_one[1])
        return carry
    lax.fori_loop(0, 4, body, 0)


def stage_two_block(src, dst, normed_ref, acc, up_ref, down_ref):
    res_f = src[...].astype(F32)
    normed_ref[...] = norm_parts(res_f)[0].astype(BF16)
    acc[...] = res_f

    def body(t, carry):
        sl = lanes(t, FWD_TILE)
        pre = dot_nn(normed_ref[...], up_ref[:, sl])
        act = (pre * gelu_parts(pre)[1]).astype(BF16)
        acc[...] += dot_nn(act, down_ref[sl, :])
        return carry
    lax.fori_loop(0, HID_TWO // FWD_TILE, body, 0)
    dst[...] = acc[...].astype(BF16)


def image_rows():
    image = lax.broadcasted_iota(jnp.int32, (8, ROWS), 0)
    row = lax.broadcasted_iota(jnp.int32, (8, ROWS), 1)
    inside = (row >= image * MERGED) & (row < (image + 1) * MERGED)
    return jnp.where(inside, 1.0, 0.0).astype(BF16)


def pooled_norm(resid):
    pooled = dot_nn(image_rows(), resid) * (1.0 / MERGED)
    return norm_parts(pooled)


UNIT = 1024
N_UNITS = 9
SHARE_ROWS = N_UNITS * UNIT
CLASS_PAD = 1024
DEVS = 8
SUBLANES = 8
LAST = N_UNITS - 1
PAIR_OUT, FIRST_OUT, SECOND_OUT, SECOND_BACK, FIRST_BACK, PAIR_BACK = range(6)


class Links:
    def __init__(self, own, final, land1, land2, sems):
        self.own, self.final, self.land1, self.land2, self.sems = own, final, land1, land2, sems
        me = lax.axis_index('data')
        self.me = me
        self.core, self.x, self.y = lax.rem(me, 2), lax.rem(me // 2, 2), me // 4
        self.pair = me + 1 - 2 * self.core
        self.x_peer = me + 2 - 4 * self.x
        self.y_peer = me + 4 - 8 * self.y

    def rows(self, unit, offset, size):
        return pl.ds(pl.multiple_of(unit * UNIT + offset, SHARD), size)

    def half(self, unit, offset, size):
        return self.rows(unit, self.core * WIDE + offset, size)

    def copy(self, unit, phase, lane, src, dst, peer):
        return pltpu.make_async_remote_copy(
            src_ref=src, dst_ref=dst, send_sem=self.sems.at[unit, phase, lane, 0], recv_sem=self.sems.at[unit, phase, lane, 1],
            device_id=(peer,), device_id_type=pl.DeviceIdType.MESH)

    def copies(self, unit, phase):
        x, y = self.x, self.y
        own, final = self.own, self.final
        if phase == PAIR_OUT:
            sl = self.rows(unit, (1 - self.core) * WIDE, WIDE)
            return [self.copy(unit, PAIR_OUT, 0, own.at[sl], final.at[sl], self.pair)]
        if phase == FIRST_OUT:
            land = lambda k: self.land1.at[pl.ds(pl.multiple_of(unit * TILE + k * WIDTH, WIDTH), WIDTH)]
            return [self.copy(unit, FIRST_OUT, 0, own.at[self.half(unit, (1 - x) * WIDTH, WIDTH)], land(0), self.x_peer),
                    self.copy(unit, FIRST_OUT, 1, own.at[self.half(unit, TILE + (1 - y) * WIDTH, WIDTH)], land(1), self.y_peer)]
        if phase == SECOND_OUT:
            land = lambda k: self.land2.at[pl.ds(pl.multiple_of(unit * WIDTH + k * SHARD, SHARD), SHARD)]
            return [self.copy(unit, SECOND_OUT, 0, own.at[self.half(unit, x * WIDTH + (1 - y) * SHARD, SHARD)], land(0), self.y_peer),
                    self.copy(unit, SECOND_OUT, 1, own.at[self.half(unit, TILE + y * WIDTH + (1 - x) * SHARD, SHARD)], land(1), self.x_peer)]
        if phase == SECOND_BACK:
            first = self.half(unit, x * WIDTH + y * SHARD, SHARD)
            second = self.half(unit, TILE + y * WIDTH + x * SHARD, SHARD)
            return [self.copy(unit, SECOND_BACK, 0, final.at[first], final.at[first], self.y_peer),
                    self.copy(unit, SECOND_BACK, 1, final.at[second], final.at[second], self.x_peer)]
        if phase == FIRST_BACK:
            first, second = self.half(unit, x * WIDTH, WIDTH), self.half(unit, TILE + y * WIDTH, WIDTH)
            return [self.copy(unit, FIRST_BACK, 0, final.at[first], final.at[first], self.x_peer),
                    self.copy(unit, FIRST_BACK, 1, final.at[second], final.at[second], self.y_peer)]
        sl = self.half(unit, 0, WIDE)
        return [self.copy(unit, PAIR_BACK, 0, final.at[sl], final.at[sl], self.pair)]

    def start(self, unit, phase):
        for copy in self.copies(unit, phase):
            copy.start()

    def wait(self, unit, phase):
        for copy in self.copies(unit, phase):
            copy.wait()

    def reduce_pair(self, unit):
        self.wait(unit, PAIR_OUT)
        x, y = self.x, self.y
        for offset in ((1 - x) * WIDTH, TILE + (1 - y) * WIDTH, x * WIDTH, TILE + y * WIDTH):
            sl = self.half(unit, offset, WIDTH)
            self.own[sl, :] = self.own[sl, :] + self.final[sl, :]
        self.start(unit, FIRST_OUT)

    def reduce_first(self, unit):
        self.wait(unit, FIRST_OUT)
        x, y = self.x, self.y
        for keep in (False, True):
            for lane, base, here, there in ((0, x * WIDTH, y, 0), (1, TILE + y * WIDTH, x, WIDTH)):
                part = here if keep else 1 - here
                sl = self.half(unit, base + part * SHARD, SHARD)
                land = pl.ds(pl.multiple_of(unit * TILE + there + part * SHARD, SHARD), SHARD)
                self.own[sl, :] = self.own[sl, :] + self.land1[land, :]
        self.start(unit, SECOND_OUT)

    def reduce_second(self, unit):
        self.wait(unit, SECOND_OUT)
        for lane, offset in ((0, self.x * WIDTH + self.y * SHARD), (1, TILE + self.y * WIDTH + self.x * SHARD)):
            sl = self.half(unit, offset, SHARD)
            land = pl.ds(pl.multiple_of(unit * WIDTH + lane * SHARD, SHARD), SHARD)
            self.final[sl, :] = self.own[sl, :] + self.land2[land, :]

    def forward(self, unit, phase):
        self.wait(unit, phase)
        self.start(unit, phase + 1)


def train_kernel(x_hbm, labels_ref, up1_hbm, dn1_hbm, mg_hbm, up2_hbm, dn2_hbm, hd_hbm,
                 sums_hbm, g_hd,
                 x_v, x_f32, st_up1, st_dn1, st_mg, st_up2, st_dn2,
                 up1, dn1, mg, up2, dn2, hd,
                 r0, r1, r2, s0, s1, normed_ref, acc, grad_a, grad_b, sems,
                 du1, dv1, own, final, land1, land2, factors, link_sems, factor_sems, out_sems):
    links = Links(own, final, land1, land2, link_sems)
    me = links.me
    st_hd = st_dn2.at[pl.ds(0, CLASSES)]
    copies = [pltpu.make_async_copy(src, dst, sems.at[i]) for i, (src, dst) in enumerate((
        (x_hbm, x_v), (up1_hbm, st_up1), (dn1_hbm, st_dn1), (mg_hbm, st_mg),
        (up2_hbm.at[0], st_up2), (dn2_hbm.at[0], st_dn2),
        (up2_hbm.at[1], st_up2), (dn2_hbm.at[1], st_dn2), (hd_hbm, st_hd)))]
    for i in range(6):
        copies[i].start()
    barrier = pltpu.get_barrier_semaphore()
    for k in range(1, DEVS):
        pl.semaphore_signal(barrier, inc=1, device_id=(lax.rem(me + k, DEVS),), device_id_type=pl.DeviceIdType.MESH)
    copies[0].wait()
    permute_tokens(x_v, x_f32, r0)
    copies[1].wait()
    copies[2].wait()
    for n in range(2):
        cast_rows(up1.at[n], st_up1.at[n], WIDTH, SHARD)
        cast_rows(dn1.at[n], st_dn1.at[n], WIDE, TILE)
    stage_one_forward(r0, r1, r2, up1, dn1)
    copies[3].wait()
    cast_rows(mg, st_mg, WIDE, SHARD)
    s0[...] = dot_nn(r2[...], mg[...]).astype(BF16)
    s2 = grad_a
    for n, (src, dst) in enumerate(((s0, s1), (s1, s2))):
        copies[4 + 2 * n].wait()
        cast_rows(up2.at[n], st_up2, WIDE, 16)
        if n == 0:
            copies[6].start()
        copies[5 + 2 * n].wait()
        cast_rows(dn2.at[n], st_dn2, 2048, SHARD)
        copies[7 + n].start()
        stage_two_block(src, dst, normed_ref, acc, up2.at[n], dn2.at[n])
    copies[8].wait()
    cast_rows(hd, st_hd, 992, 32)
    hd[992:CLASSES, :] = st_hd[992:CLASSES, :].astype(BF16)
    hd[CLASSES:, :] = jnp.zeros((CLASS_PAD - CLASSES, WIDE), BF16)
    head_normed, head_rstd = pooled_norm(s2[...])
    head_b = head_normed.astype(BF16)
    class_id = lax.broadcasted_iota(jnp.int32, (SUBLANES, CLASS_PAD), 1)
    real_row = lax.broadcasted_iota(jnp.int32, (SUBLANES, CLASS_PAD), 0) < IMGS
    logits = jnp.where(class_id < CLASSES, dot_nt(head_b, hd[...]), -jnp.inf)
    top = jnp.max(logits, axis=-1, keepdims=True)
    expd = jnp.exp(logits - top)
    probs = expd / jnp.sum(expd, axis=-1, keepdims=True)
    onehot = jnp.where(class_id == labels_ref[...], 1.0, 0.0)
    grad_logits = jnp.where(real_row, (probs - onehot) * (1.0 / (IMGS * DEVS)), 0.0).astype(BF16)
    factors[me, :, :WIDE] = head_b
    factors[me, :, WIDE:] = grad_logits
    grad_pooled = norm_back(dot_nn(grad_logits, hd[...]), head_normed, head_rstd) * (1.0 / MERGED)
    grad_a[...] = dot_tn(image_rows(), grad_pooled.astype(BF16)).astype(BF16)

    pl.semaphore_wait(barrier, DEVS - 1)

    def factor_copy(k):
        return pltpu.make_async_remote_copy(
            src_ref=factors.at[me], dst_ref=factors.at[me], send_sem=factor_sems.at[k, 0], recv_sem=factor_sems.at[k, 1],
            device_id=(lax.rem(me + k, DEVS),), device_id_type=pl.DeviceIdType.MESH)

    grads = (grad_a, grad_b)
    for step, n in enumerate((1, 0)):
        g_in, g_out = grads[step], grads[1 - step]
        src = (s0, s1)[n]
        normed_ref[...] = norm_parts(src[...].astype(F32))[0].astype(BF16)
        acc[...] = jnp.zeros_like(acc)

        def tile(t, row, n=n, g_in=g_in):
            sl = lanes(t, TILE)
            pre = dot_nn(normed_ref[...], up2[n, :, sl])
            square, half = gelu_parts(pre)
            act = (pre * half).astype(BF16)
            grad_pre = (gelu_slope(pre, square, half) * dot_nt(g_in[...], dn2[n, sl, :])).astype(BF16)
            own[pl.ds(row + TILE, TILE), :] = dot_tn(act, g_in[...]).astype(BF16)
            grad_up = dot_tn(normed_ref[...], grad_pre).astype(BF16)
            own[pl.ds(row, TILE), :TILE] = grad_up[:TILE]
            own[pl.ds(row, TILE), TILE:] = grad_up[TILE:]
            acc[...] += dot_nt(grad_pre, up2[n, :, sl])

        def body(p, carry, step=step, tile=tile):
            unit = step * 4 + p
            row = pl.multiple_of(unit * UNIT, UNIT)

            def guarded(lag, action):
                if step:
                    action(unit - lag)
                else:
                    @pl.when(p >= lag)
                    def _():
                        action(unit - lag)

            tile(2 * p, row)
            guarded(1, links.reduce_pair)
            tile(2 * p + 1, row + WIDE)
            guarded(3, links.reduce_second)
            guarded(2, links.reduce_first)
            links.start(unit, PAIR_OUT)
            return carry
        if step == 0:
            for k in range(1, DEVS):
                factor_copy(k).start()
        lax.fori_loop(0, N_TILES // 2, body, 0)
        normed_f, rstd = norm_parts(src[...].astype(F32))
        g_out[...] = (norm_back(acc[...], normed_f, rstd) + g_in[...].astype(F32)).astype(BF16)
    own[LAST * UNIT:LAST * UNIT + WIDE, :] = dot_tn(r2[...], grad_a[...]).astype(BF16)
    grad_b[...] = dot_nt(grad_a[...], mg[...]).astype(BF16)

    links.reduce_pair(7)
    for unit in range(5):
        links.start(unit, SECOND_BACK)

    def in_layer_one():
        links.reduce_second(5)
        links.reduce_first(6)
        links.start(5, SECOND_BACK)

    def in_layer_zero():
        links.reduce_second(6)
        links.reduce_first(7)
        links.start(6, SECOND_BACK)

    for n, src, g_in, g_out, between in ((1, r1, grad_b, grad_a, in_layer_one), (0, r0, grad_a, grad_b, in_layer_zero)):
        du1[...] = jnp.zeros_like(du1)
        dv1[...] = jnp.zeros_like(dv1)

        def body(j, carry, n=n, src=src, g_in=g_in, g_out=g_out, between=between):
            sl = lanes(j, WIDTH)
            normed_f, rstd = norm_parts(src[:, sl].astype(F32))
            normed = normed_f.astype(BF16)
            grad = g_in[:, sl]
            pre = dot_nn(normed, up1[n])
            square, half = gelu_parts(pre)
            act = (pre * half).astype(BF16)
            grad_pre = (gelu_slope(pre, square, half) * dot_nt(grad, dn1[n])).astype(BF16)
            dv1[...] += dot_tn(grad, act)
            du1[...] += dot_tn(normed, grad_pre)
            if n:
                back = norm_back(dot_nt(grad_pre, up1[n]), normed_f, rstd)
                g_out[:, sl] = (back + grad.astype(F32)).astype(BF16)
            pl.when(j == 1)(between)
            return carry
        lax.fori_loop(0, 4, body, 0)
        base = LAST * UNIT + WIDE + n * WIDTH
        own[base:base + WIDTH, :] = du1[...].astype(BF16)
        own[base + TILE:base + TILE + WIDTH, :] = dv1[...].astype(BF16)
        for unit in (range(2) if n else range(2, 4)):
            links.forward(unit, SECOND_BACK)
    links.start(LAST, PAIR_OUT)

    for k in range(1, DEVS):
        factor_copy(k).wait()

    def head_tile(c, carry):
        sl = pl.ds(pl.multiple_of(WIDE + c * WIDTH, WIDTH), WIDTH)
        total = jnp.zeros((WIDTH, WIDE), F32)
        for d in range(DEVS):
            total += dot_tn(factors[d, :, sl], factors[d, :, :WIDE]).astype(BF16).astype(F32)
        g_hd[pl.ds(pl.multiple_of(c * WIDTH, WIDTH), WIDTH), :] = total.astype(BF16)
        return carry
    lax.fori_loop(0, CLASS_PAD // WIDTH, head_tile, 0)

    def out_copy(unit):
        sl = pl.ds(unit * UNIT, UNIT)
        return pltpu.make_async_copy(final.at[sl], sums_hbm.at[sl], out_sems.at[unit])

    def finish(unit):
        links.wait(unit, PAIR_BACK)
        out_copy(unit).start()

    links.reduce_pair(LAST)
    links.reduce_second(7)
    links.forward(4, SECOND_BACK)
    links.forward(5, SECOND_BACK)
    links.start(7, SECOND_BACK)
    links.reduce_first(LAST)
    for unit in range(4):
        links.forward(unit, FIRST_BACK)
    links.forward(6, SECOND_BACK)
    links.reduce_second(LAST)
    links.forward(7, SECOND_BACK)
    links.start(LAST, SECOND_BACK)
    for unit in range(4, 6):
        links.forward(unit, FIRST_BACK)
    for unit in range(4):
        finish(unit)
    links.forward(6, FIRST_BACK)
    links.forward(LAST, SECOND_BACK)
    links.forward(7, FIRST_BACK)
    links.forward(LAST, FIRST_BACK)
    for unit in range(4, N_UNITS):
        finish(unit)
    for unit in range(N_UNITS):
        out_copy(unit).wait()


def sum_rows(tile):
    rows, cols = tile.shape
    return jnp.sum(tile.reshape(rows // 8, 8, cols), axis=0)


def lars_matrix(steps, piece, cols, tails=()):
    zero = jnp.zeros((8, cols), F32)

    def norms(i, carry):
        w, _, g, _ = piece(i)
        w, g = w[...], g[...].astype(F32)
        return carry[0] + sum_rows(w * w), carry[1] + sum_rows(g * g)
    w_acc, g_acc = lax.fori_loop(0, steps, norms, (zero, zero))
    for w, _, g, _ in tails:
        w, g = w[...], g[...].astype(F32)
        w_acc, g_acc = w_acc + sum_rows(w * w), g_acc + sum_rows(g * g)
    w_norm = jnp.sqrt(jnp.sum(jnp.sum(w_acc, axis=0, keepdims=True), axis=1, keepdims=True))
    g_norm = jnp.sqrt(jnp.sum(jnp.sum(g_acc, axis=0, keepdims=True), axis=1, keepdims=True))
    scale = TRUST * (w_norm / g_norm)

    def update_piece(w, v, g, b):
        new_v = MOMENTUM * v[...] + scale * g[...].astype(F32)
        new_w = w[...] - new_v
        v[...] = new_v
        w[...] = new_w
        b[...] = new_w.astype(BF16)

    def update(i, carry):
        update_piece(*piece(i))
        return carry
    lax.fori_loop(0, steps, update, 0)
    for tail in tails:
        update_piece(*tail)


def row_pieces(w, v, g, b, step):
    def piece(i):
        sl = pl.ds(pl.multiple_of(i * step, step), step)
        return w.at[sl], v.at[sl], g.at[sl], b.at[sl]
    return piece


def up_pieces(w, v, g, b):
    def piece(i):
        h, part = i // 2, lax.rem(i, 2)
        rows, cols = lanes(part, 256), lanes(h, 256)
        g_rows = pl.ds(pl.multiple_of(h * 512, 512), 256)
        return w.at[rows, cols], v.at[rows, cols], g.at[g_rows, rows], b.at[rows, cols]
    return piece


def down_pieces(w, v, g, b):
    def piece(i):
        h, part = i // 2, lax.rem(i, 2)
        rows = pl.ds(pl.multiple_of(i * 128, 128), 128)
        g_rows = pl.ds(pl.multiple_of(h * 512 + 256 + part * 128, 128), 128)
        return w.at[rows], v.at[rows], g.at[g_rows], b.at[rows]
    return piece


def next_kernel(x_hbm, up1_hbm, dn1_hbm, mg_hbm, up2_hbm, dn2_hbm, hd_hbm,
                vup1_hbm, vdn1_hbm, vmg_hbm, vup2_hbm, vdn2_hbm, vhd_hbm, sums_hbm, ghd_hbm,
                logits_ref, o_up1, o_dn1, o_mg, o_up2, o_dn2, o_hd, ov_up1, ov_dn1, ov_mg, ov_up2, ov_dn2, ov_hd,
                x_v, x_f32, wb_up1, wb_dn1, wb_mg, wb_up2, wb_dn2, wb_hd, vb_up1, vb_dn1, vb_mg, vb_up2, vb_dn2, vb_hd,
                gb_small, gb_turn, gb_two, gb_hd,
                up1, dn1, mg, up2, dn2, hd, r0, s0, s1, normed_ref, acc, sem_in, sem_out, sem_g):
    jobs = {}
    for n in range(2):
        jobs['up1', n] = (up1_hbm.at[n], vup1_hbm.at[n], o_up1.at[n], ov_up1.at[n], wb_up1.at[n], vb_up1.at[n])
        jobs['dn1', n] = (dn1_hbm.at[n], vdn1_hbm.at[n], o_dn1.at[n], ov_dn1.at[n], wb_dn1.at[n], vb_dn1.at[n])
        jobs['up2', n] = (up2_hbm.at[n], vup2_hbm.at[n], o_up2.at[n], ov_up2.at[n], wb_up2, vb_up2)
        jobs['dn2', n] = (dn2_hbm.at[n], vdn2_hbm.at[n], o_dn2.at[n], ov_dn2.at[n], wb_dn2, vb_dn2)
    jobs['mg', 0] = (mg_hbm, vmg_hbm, o_mg, ov_mg, wb_mg, vb_mg)
    jobs['hd', 0] = (hd_hbm, vhd_hbm, o_hd, ov_hd, wb_hd, vb_hd)
    order = {key: i for i, key in enumerate(jobs)}

    def loads(*key):
        w, v, _, _, wb, vb = jobs[key]
        return [pltpu.make_async_copy(w, wb, sem_in.at[order[key], 0]), pltpu.make_async_copy(v, vb, sem_in.at[order[key], 1])]

    def stores(*key):
        _, _, ow, ov, wb, vb = jobs[key]
        return [pltpu.make_async_copy(wb, ow, sem_out.at[order[key], 0]), pltpu.make_async_copy(vb, ov, sem_out.at[order[key], 1])]

    def each(copies, action):
        for copy in copies:
            getattr(copy, action)()

    small = pltpu.make_async_copy(sums_hbm.at[pl.ds(LAST * UNIT, UNIT)], gb_small, sem_g.at[0])
    two = [pltpu.make_async_copy(sums_hbm.at[pl.ds((1 - n) * 4 * UNIT, 4 * UNIT)], gb_two.at[n], sem_g.at[1 + n]) for n in range(2)]
    head = pltpu.make_async_copy(ghd_hbm, gb_hd, sem_g.at[3])
    x_copy = pltpu.make_async_copy(x_hbm, x_v, sem_g.at[4])
    x_copy.start()
    small.start()
    for key in (('up1', 0), ('dn1', 0), ('up1', 1), ('dn1', 1), ('mg', 0)):
        each(loads(*key), 'start')
    two[0].start()
    each(loads('up2', 0), 'start')
    each(loads('dn2', 0), 'start')
    two[1].start()
    head.start()
    each(loads('hd', 0), 'start')
    x_copy.wait()
    permute_tokens(x_v, x_f32, r0)
    small.wait()
    for n in range(2):
        each(loads('up1', n), 'wait')
        lars_matrix(2, row_pieces(wb_up1.at[n], vb_up1.at[n], gb_small.at[pl.ds(512 + n * 128, 128)], up1.at[n], 64), 512)
        each(stores('up1', n), 'start')
        each(loads('dn1', n), 'wait')
        gb_turn[...] = gb_small[pl.ds(768 + n * 128, 128), :].astype(F32).T
        lars_matrix(4, row_pieces(wb_dn1.at[n], vb_dn1.at[n], gb_turn, dn1.at[n], 128), 128)
        each(stores('dn1', n), 'start')
    stage_one_forward(r0, s0, s1, up1, dn1)
    each(loads('mg', 0), 'wait')
    lars_matrix(8, row_pieces(wb_mg, vb_mg, gb_small.at[pl.ds(0, 512)], mg, 64), 512)
    each(stores('mg', 0), 'start')
    s0[...] = dot_nn(s1[...], mg[...]).astype(BF16)

    def head_step():
        head.wait()
        each(loads('hd', 0), 'wait')
        tail = pl.ds(992, 8)
        lars_matrix(31, row_pieces(wb_hd, vb_hd, gb_hd, hd, 32), 512, [(wb_hd.at[tail], vb_hd.at[tail], gb_hd.at[tail], hd.at[tail])])
        each(stores('hd', 0), 'start')

    for n, (src, dst) in enumerate(((s0, s1), (s1, s0))):
        two[n].wait()
        each(loads('up2', n), 'wait')
        lars_matrix(16, up_pieces(wb_up2, vb_up2, gb_two.at[n], up2), 256)
        each(stores('up2', n), 'start')
        each(loads('dn2', n), 'wait')
        lars_matrix(16, down_pieces(wb_dn2, vb_dn2, gb_two.at[n], dn2), 512)
        each(stores('dn2', n), 'start')
        if n == 0:
            head_step()
            for name in ('up2', 'dn2'):
                each(stores(name, 0), 'wait')
                each(loads(name, 1), 'start')
        stage_two_block(src, dst, normed_ref, acc, up2, dn2)
    head_b = pooled_norm(s0[...])[0].astype(BF16)
    logits_ref[...] = dot_nt(head_b, hd[...])[:IMGS]
    for key in jobs:
        if key not in (('up2', 0), ('dn2', 0)):
            each(stores(*key), 'wait')


W_SHAPES = ((2, 128, 512), (2, 512, 128), (512, 512), (2, 512, 2048), (2, 2048, 512), (CLASSES, 512))
BUF_SHAPES = W_SHAPES[:3] + ((512, 2048), (2048, 512), (CLASSES, 512))


def vmem(shape, dtype):
    return pltpu.VMEM(shape, dtype)


ANY_SPEC = pl.BlockSpec(memory_space=pl.ANY)
VMEM_SPEC = pl.BlockSpec(memory_space=pltpu.VMEM)


def run_train(x_now, labels, params):
    act = lambda dt=BF16: vmem((ROWS, WIDE), dt)
    dma = pltpu.SemaphoreType.DMA
    return pl.pallas_call(
        train_kernel,
        out_shape=[jax.ShapeDtypeStruct((SHARE_ROWS, WIDE), BF16), jax.ShapeDtypeStruct((CLASS_PAD, WIDE), BF16)],
        in_specs=[ANY_SPEC, VMEM_SPEC] + [ANY_SPEC] * 6,
        out_specs=[ANY_SPEC, VMEM_SPEC],
        scratch_shapes=[vmem((ROWS * 4, WIDTH), BF16), vmem((ROWS * 4, WIDTH), F32)]
        + [vmem(shape, F32) for shape in BUF_SHAPES[:5]] + [vmem(shape, BF16) for shape in W_SHAPES[:5]] + [vmem((CLASS_PAD, WIDE), BF16)]
        + [act()] * 6 + [act(F32), act(), act(), dma((9,)), vmem((128, 512), F32), vmem((128, 512), F32)]
        + [vmem((SHARE_ROWS, WIDE), BF16), vmem((SHARE_ROWS, WIDE), BF16), vmem((N_UNITS * 256, WIDE), BF16), vmem((N_UNITS * 128, WIDE), BF16)]
        + [vmem((DEVS, 8, WIDE + CLASS_PAD), BF16), dma((N_UNITS, 6, 2, 2)), dma((DEVS, 2)), dma((N_UNITS,))],
        compiler_params=pltpu.CompilerParams(vmem_limit_bytes=66_000_000, collective_id=0, has_side_effects=True),
        cost_estimate=pl.CostEstimate(flops=30_000_000_000, bytes_accessed=40_000_000, transcendentals=0),
        name='train_part',
    )(x_now, labels, *params)


def run_next(x_next, params, velocities, sums, head_sum):
    act = lambda dt=BF16: vmem((ROWS, WIDE), dt)
    dma = pltpu.SemaphoreType.DMA
    outs = [jax.ShapeDtypeStruct((IMGS, CLASSES), F32)] + [jax.ShapeDtypeStruct(shape, F32) for shape in W_SHAPES] * 2
    return pl.pallas_call(
        next_kernel,
        out_shape=outs,
        in_specs=[ANY_SPEC] * 15,
        out_specs=[VMEM_SPEC] + [ANY_SPEC] * 12,
        scratch_shapes=[vmem((ROWS * 4, WIDTH), BF16), vmem((ROWS * 4, WIDTH), F32)]
        + [vmem(shape, F32) for shape in BUF_SHAPES] * 2
        + [vmem((UNIT, WIDE), BF16), vmem((512, 128), F32), vmem((2, 4 * UNIT, WIDE), BF16), vmem((CLASS_PAD, WIDE), BF16)]
        + [vmem(shape, BF16) for shape in BUF_SHAPES]
        + [act()] * 4 + [act(F32), dma((10, 2)), dma((10, 2)), dma((5,))],
        compiler_params=pltpu.CompilerParams(vmem_limit_bytes=VMEM_BYTES),
        cost_estimate=pl.CostEstimate(flops=10_000_000_000, bytes_accessed=100_000_000, transcendentals=0),
        name='next_part',
    )(x_next, *params, *velocities, sums, head_sum)


def turn_head(arrays):
    return tuple(arrays[:5]) + (arrays[5].T,)


def solution(mesh):
    def local_step(x_now, labels_now, x_next, *weights):
        params, velocities = turn_head(weights[:6]), turn_head(weights[6:])
        labels = jnp.pad(labels_now, (0, 8 - IMGS)).reshape(8, 1)
        sums, head_sum = run_train(x_now.reshape(ROWS * 4, WIDTH), labels, params)
        outs = run_next(x_next.reshape(ROWS * 4, WIDTH), params, velocities, sums, head_sum)
        return (outs[0],) + turn_head(outs[1:7]) + turn_head(outs[7:])

    split = P('data')
    in_specs = (split, split, split) + (P(),) * 12
    out_specs = (split,) + (P(),) * 12
    return jax.shard_map(local_step, mesh=mesh, in_specs=in_specs, out_specs=out_specs, check_vma=False)
```

time: 282 us -> 163 us (0.58)
  waiting for transfers between devices: 137 us -> 0 us
  Pallas kernels: 118 us -> 161 us
  between operations: 14.1 us -> 0.84 us
  local copies, waits for them, and re-layouts: 12.4 us -> 1.33 us
    psum x1 -> x0, waiting for transfers between devices: 137 us -> none  [local_step(): sums = lax.psum(tuple(grads), 'data')]
    pallas_call x2, Pallas kernels: 118 us -> 161 us  [the longest x1 121 us: run_train(): pl.pallas_call(train_kernel, out_shape=[jax.ShapeDtypeStruct((SHARE_ROWS,...]
    unnamed x6 -> x0, local copies, waits for them, and re-layouts: 6.3 us -> none
    pallas_call x2 -> x0, local copies, waits for them, and re-layouts: 4.79 us -> none  [run_next(): pl.pallas_call(next_kernel, out_shape=outs, in_specs=[ANY_SPEC] * 19, out...]
  transfers between devices with their start and end apart: 1 -> 0, of which waited for: 1 -> 0; matrix products, arithmetic and copies ran while one was open for 1% -> 0% of each run, Pallas kernels for 0% -> 0%
where the time goes in v2:
time: 163 us
  Pallas kernels  161 us (99%)
    pallas_call x1, Pallas kernels, run_train(): pl.pallas_call(train_kernel, out_shape=[jax.ShapeDtypeStruct((SHARE_ROWS,...  121 us
    pallas_call x1, Pallas kernels, run_next(): pl.pallas_call(next_kernel, out_shape=outs, in_specs=[ANY_SPEC] * 15, out...  39.9 us

profile of v2, /device:TPU:0, one launch (start us, length us, event | category | flops | bytes accessed | tf_op | source)
XLA Modules:
  0.0 162.9 jit_solution(4507014266921211921)
XLA Ops:
  0.6 0.7 pad_bitcast_fusion
  1.3 0.7 copy.28.labels_ref
  2.0 120.8 %train_part.1 = (bf16[9216,512]{1,0:T(8,128)(2,1)}, bf16[1024,512]{1,0:T(8,128)(2,1)}) custom-call(bf16[3136,128]{1,0:T(8,128)(2,1)} %bitcast.14, s32[8,1]{1,0:T(8,128)} %copy.28.labels_ref, f32[2,128,512]{2,1,0:T(8,128)} %up1_hbm.3, f32[2,512,128]{2,1,0:T(8,128)} %dn1_hbm.3, f32[512,512]{1,0:T(8,128)} %mg_hbm.3, f32[2,512,2048]{2,1,0:T(8,128)} %up2_hbm.3, ...), custom_call_target="tpu_custom_call" | custom-call | flops 30000001024 | bytes 40000000 | tf_op jit(solution)/shard_map/train_part/pallas_call | solution.py:585
  122.8 39.9 %next_part.1 = (f32[4,1000]{1,0:T(4,128)}, f32[2,128,512]{2,1,0:T(8,128)}, f32[2,512,128]{2,1,0:T(8,128)}, f32[512,512]{1,0:T(8,128)}, f32[2,512,2048]{2,1,0:T(8...) custom-call(bf16[3136,128]{1,0:T(8,128)(2,1)} %bitcast.11, ...), custom_call_target="tpu_custom_call" | custom-call | flops 10000000000 | bytes 100000000 | tf_op jit(solution)/shard_map/next_part/pallas_call | solution.py:605
